TPU v7x, 32 devices: a whole 2x2x4 slice. The times are simulated.
32 devices in a mesh: dp: 16 (over z, y, core), tensor: 2 (over x).
Axes of the slice: x: 2, y: 2, z: 4, core: 2. Of those that a mesh axis runs over, the one named last changes fastest.
Arguments:
- expert_act: bfloat16 [16384, 2880], P(('dp', 'tensor')), may hold values from -6 to 6
- grad_out: bfloat16 [32768, 1440], P(('dp', 'tensor')), may hold values from -6 to 6
- slot_token: int32 [16384], P(('dp', 'tensor')), may hold values from 0 to 1023, as said below
- slot_prob: float32 [16384], P(('dp', 'tensor')), may hold values from 0.2 to 1
- live_count: int32 [32], P(('dp', 'tensor')), may hold values from 128 to 512, as said below
Outputs:
- weight_grad: float32 [2880, 1440], P('dp', 'tensor')
Inputs may be any that keep to these rules, and one draw needn't show every extreme that they name: `slot_token`: each device's 512 entries are distinct token indices of that device. `live_count`: each entry is 512 // j for some j of 1 to 4.
All inputs are finite; a program needn't handle non-finite values.
Results may differ from a plain program's by a relative error of at most 0.0029.
Values may be sent and summed in bfloat16 or wider, within the bound.
No kernel may reach another device: no remote copies, remote signals or barrier semaphores. Data moves between devices by JAX's collectives and lax.ppermute only.
A program may use at most 128 MiB of HBM per device.

v0:
```python
import math
import jax
import jax.numpy as jnp
from jax import lax
from jax.sharding import PartitionSpec as P


def contract(left, right):
    return lax.dot_general(
        left, right, (((0,), (0,)), ((), ())), preferred_element_type=jnp.float32
    )


def shards(expert_act, grad_out, slot_token, slot_prob, live_count):
    slot_count = expert_act.shape[0]
    devices = lax.axis_size("dp") * lax.axis_size("tensor")
    scaling = 1.0 / math.sqrt(slot_count * devices)
    position = jnp.arange(slot_count, dtype=jnp.int32)
    live_mask = position < live_count[0]
    weighting = jnp.where(live_mask, slot_prob, jnp.zeros_like(slot_prob))
    picked = jnp.take(grad_out, slot_token, axis=0).astype(jnp.float32)
    weighted = (picked * weighting[:, None]).astype(jnp.bfloat16)
    both_acts = lax.all_gather(expert_act, "tensor", axis=0, tiled=True)
    both_grads = lax.all_to_all(weighted, "tensor", split_axis=1, concat_axis=0, tiled=True)
    gradient = lax.psum_scatter(
        contract(both_acts, both_grads), "dp", scatter_dimension=0, tiled=True
    )
    return gradient * scaling


def solution(mesh):
    return jax.shard_map(
        shards,
        mesh=mesh,
        in_specs=(
            P(("dp", "tensor"), None),
            P(("dp", "tensor"), None),
            P(("dp", "tensor")),
            P(("dp", "tensor")),
            P(("dp", "tensor")),
        ),
        out_specs=P("dp", "tensor"),
        check_vma=False,
    )
```

profile of v0, /device:TPU:0, one launch (start us, length us, event | category | flops | bytes accessed | tf_op | source)
XLA Modules:
  0.0 293.3 jit_solution(11381292390871192183)
XLA Ops:
  6.5 0.0 all-gather.2.cloned.1.call-start
  6.5 0.7 all-gather.2.cloned.1.call-update
  7.3 0.0 copy-start
  7.3 0.0 all-reduce.3.cloned.1.call-start
  7.3 3.1 %copy.16 = bf16[1024,1440]{1,0:T(8,128)(2,1)S(1)} copy(bf16[1024,1440]{0,1:T(8,128)(2,1)} %param.6) | data formatting | bytes 5898240 | tf_op args[1]
  10.5 0.0 copy-done
  10.5 3.0 %gather_fusion = bf16[512,1440]{1,0:T(8,128)(2,1)} fusion(bf16[1024,1440]{1,0:T(8,128)(2,1)S(1)} %copy.16, s32[1024]{0:T(1024)S(1)} %pad_clamp_fusion), kind=kCustom, calls=%fused_computation | custom fusion | bytes 2951168 | tf_op jit(solution)/shard_map/jit(_take)/gather | solution.py:21
  13.5 0.0 copy-start.1
  13.5 1.7 copy.17
  15.8 0.0 copy-done.1
  15.9 0.4 multiply_convert_fusion
  16.3 37.9 %all_to_all.16 = bf16[512,2,720]{0,2,1:T(8,128)(2,1)S(1)} all-to-all(bf16[512,2,720]{0,2,1:T(8,128)(2,1)S(1)} %multiply_convert_fusion), channel_id=1, replica_groups=mesh['dp'=16,'tensor'=2] {'tensor'}, dimensions={1} | all-to-all | bytes 2949120 | tf_op jit(solution)/shard_map/all_to_all | solution.py:24
  54.1 0.2 copy.22
  54.3 47.6 %all-gather.2.cloned.1.call-done = bf16[1024,2880]{0,1:T(8,128)(2,1)} async-done(((bf16[512,2880]{0,1:T(8,128)(2,1)}), bf16[1024,2880]{0,1:T(8,128)(2,1)}) %all-gather.2.cloned.1.call-update) | async-done | bytes 5898256 | tf_op jit(solution)/shard_map/all_gather | solution.py:23
  101.9 9.6 %convolution_bitcast_fusion = f32[2880,720]{0,1:T(8,128)} fusion(bf16[1024,720]{0,1:T(8,128)(2,1)S(1)} %bitcast.15, bf16[1024,2880]{0,1:T(8,128)(2,1)} %all-gather.2.cloned.1.call-done), kind=kOutput, calls=%fused_computation.1 | convolution fusion | flops 4246732800 | bytes 15667200 | tf_op jit(solution)/shard_map/dot_general | solution.py:9
  111.5 0.0 copy-start.2
  111.5 0.0 all-reduce.3.cloned.1.call-update
  111.6 0.6 copy-done.2
  112.2 0.6 dynamic-slice
  113.4 170.4 %all-reduce.3.cloned.1.call-done = f32[2880,720]{0,1:T(8,128)} async-done(((f32[2880,720]{0,1:T(8,128)}), f32[2880,720]{0,1:T(8,128)}) %all-reduce.3.cloned.1.call-update) | async-done | bytes 8294416
  283.8 1.5 constant_dynamic-slice_fusion
  285.3 0.2 copy.19
  285.6 0.8 broadcast_multiply_fusion
  (4 shorter events, 0.0 us)
Async XLA Ops:
  6.5 95.4 %all-gather.2.cloned.1.call-start = ((), (), s32[]{:S(2)}) async-start(), calls=%async_computation.1 | async-start | bytes 8847360 | tf_op jit(solution)/shard_map/all_gather | solution.py:23
  7.3 3.2 %copy-start = (s32[512]{0:T(512)S(1)}, s32[512]{0:T(512)}, u32[]{:S(2)}) copy-start(s32[512]{0:T(512)} %param.7) | copy-start | bytes 6148
  7.3 276.6 %all-reduce.3.cloned.1.call-start = ((), (), s32[]{:S(2)}) async-start(), calls=%async_computation.2 | async-start | bytes 16957440
  13.5 2.4 copy-start.1
  111.5 0.7 copy-start.2
Sparse Core Ops, SparseCore 0:
  8.9 92.9 all-gather.1
  111.7 172.0 all-reduce.2
where the time goes:
time: 294 us; the launch traced here: 293 us
  waiting for transfers between devices  219 us (74%)
  blocking collectives  37.9 us (13%)
  between operations  14.8 us (5%)
  local copies, waits for them, and re-layouts  10.9 us (4%)
  matrix products  9.64 us (3%)
    unnamed x3, waiting for transfers between devices  171 us
    all_gather x1, waiting for transfers between devices, shards(): both_acts = lax.all_gather(expert_act, 'tensor', axis=0, tiled=True)  47.6 us
    all_to_all x1, blocking collectives, shards(): lax.all_to_all(weighted, 'tensor', split_axis=1, concat_axis=0, tiled=True)  37.9 us
    dot_general x1, matrix products, contract(): lax.dot_general(left, right, (((0,), (0,)), ((), ())), preferred_element_...  9.64 us
  transfers between devices with their start and end apart: 2, of which 2 were waited for; matrix products, arithmetic and copies ran while one was open for 3% of the time, Pallas kernels for 0%

commit v1 on v0

--- a/solution.py
+++ b/solution.py
@@ -21,7 +21,13 @@
     picked = jnp.take(grad_out, slot_token, axis=0).astype(jnp.float32)
     weighted = (picked * weighting[:, None]).astype(jnp.bfloat16)
     both_acts = lax.all_gather(expert_act, "tensor", axis=0, tiled=True)
-    both_grads = lax.all_to_all(weighted, "tensor", split_axis=1, concat_axis=0, tiled=True)
+    resolve_the_rings = lambda a0, along_dim, pos_dim: jnp.concatenate(
+        lax.all_to_all(
+            jnp.stack(jnp.split(a0, lax.axis_size("tensor"), along_dim), 0), "tensor", 0, 0
+        ),
+        pos_dim,
+    )
+    both_grads = resolve_the_rings(weighted, 1, 0)
     gradient = lax.psum_scatter(
         contract(both_acts, both_grads), "dp", scatter_dimension=0, tiled=True
     )

time: 294 us -> 295 us (level)
  no operation moved by 1% of the time
where the time goes in v1:
time: 295 us; the launch traced here: 294 us
  waiting for transfers between devices  218 us (74%)
  blocking collectives  38.5 us (13%)
  between operations  14.8 us (5%)
  local copies, waits for them, and re-layouts  10.4 us (4%)
  matrix products  9.65 us (3%)
    unnamed x3, waiting for transfers between devices  171 us
    all_gather x1, waiting for transfers between devices, shards(): both_acts = lax.all_gather(expert_act, 'tensor', axis=0, tiled=True)  47 us
    all_to_all x1, blocking collectives, shards(): lax.all_to_all(jnp.stack(jnp.split(a0, lax.axis_size('tensor'), along_dim...  38.5 us
    dot_general x1, matrix products, contract(): lax.dot_general(left, right, (((0,), (0,)), ((), ())), preferred_element_...  9.65 us
  transfers between devices with their start and end apart: 2, of which 2 were waited for; matrix products, arithmetic and copies ran while one was open for 3% of the time, Pallas kernels for 0%

profile of v1, /device:TPU:0, one launch (start us, length us, event | category | flops | bytes accessed | tf_op | source)
XLA Modules:
  0.0 294.2 jit_solution(1808262338059684149)
XLA Ops:
  6.5 0.0 all-gather.2.cloned.1.call-start
  6.5 0.7 all-gather.2.cloned.1.call-update
  7.3 0.0 copy-start
  7.3 0.0 all-reduce.3.cloned.1.call-start
  7.3 3.1 %copy.15 = bf16[1024,1440]{1,0:T(8,128)(2,1)S(1)} copy(bf16[1024,1440]{0,1:T(8,128)(2,1)} %param.6) | data formatting | bytes 5898240 | tf_op args[1]
  11.1 0.0 copy-done
  11.1 0.0 copy-start.1
  11.2 3.0 %gather_fusion = bf16[512,1440]{1,0:T(8,128)(2,1)} fusion(bf16[1024,1440]{1,0:T(8,128)(2,1)S(1)} %copy.15, s32[1024]{0:T(1024)S(1)} %pad_clamp_fusion), kind=kCustom, calls=%fused_computation | custom fusion | bytes 2951168 | tf_op jit(solution)/shard_map/jit(_take)/gather | solution.py:21
  14.1 0.0 copy-done.1
  14.2 1.8 multiply_convert_fusion
  16.0 0.5 slice_bitcast_fusion.1
  16.5 0.2 pad_maximum_fusion
  16.6 0.7 copy.16
  17.3 38.5 %all_to_all.5 = bf16[2,512,720]{1,2,0:T(8,128)(2,1)S(1)} all-to-all(bf16[2,512,720]{1,2,0:T(8,128)(2,1)S(1)} %copy.16), channel_id=1, replica_groups=mesh['dp'=16,'tensor'=2] {'tensor'}, dimensions={0} | all-to-all | bytes 2949120 | tf_op jit(solution)/shard_map/all_to_all | solution.py:25
  55.8 0.2 copy.21
  56.0 47.0 %all-gather.2.cloned.1.call-done = bf16[1024,2880]{0,1:T(8,128)(2,1)} async-done(((bf16[512,2880]{0,1:T(8,128)(2,1)}), bf16[1024,2880]{0,1:T(8,128)(2,1)}) %all-gather.2.cloned.1.call-update) | async-done | bytes 5898256 | tf_op jit(solution)/shard_map/all_gather | solution.py:23
  103.0 9.7 %convolution_bitcast_fusion = f32[2880,720]{0,1:T(8,128)} fusion(bf16[1024,720]{0,1:T(8,128)(2,1)S(1)} %bitcast.16, bf16[1024,2880]{0,1:T(8,128)(2,1)} %all-gather.2.cloned.1.call-done), kind=kOutput, calls=%fused_computation.1 | convolution fusion | flops 4246732800 | bytes 15667200 | tf_op jit(solution)/shard_map/dot_general | solution.py:9
  112.6 0.0 all-reduce.3.cloned.1.call-update
  112.6 0.6 copy-done.2
  113.3 0.6 dynamic-slice
  114.5 170.3 %all-reduce.3.cloned.1.call-done = f32[2880,720]{0,1:T(8,128)} async-done(((f32[2880,720]{0,1:T(8,128)}), f32[2880,720]{0,1:T(8,128)}) %all-reduce.3.cloned.1.call-update) | async-done | bytes 8294416
  284.8 1.5 constant_dynamic-slice_fusion
  286.3 0.2 copy.18
  286.5 0.8 broadcast_multiply_fusion
  (5 shorter events, 0.0 us)
Async XLA Ops:
  6.5 96.4 %all-gather.2.cloned.1.call-start = ((), (), s32[]{:S(2)}) async-start(), calls=%async_computation.1 | async-start | bytes 8847360 | tf_op jit(solution)/shard_map/all_gather | solution.py:23
  7.3 3.9 %copy-start = (s32[512]{0:T(512)S(1)}, s32[512]{0:T(512)}, u32[]{:S(2)}) copy-start(s32[512]{0:T(512)} %param.7) | copy-start | bytes 6148
  7.3 277.5 %all-reduce.3.cloned.1.call-start = ((), (), s32[]{:S(2)}) async-start(), calls=%async_computation.2 | async-start | bytes 16957440
  11.1 3.0 %copy-start.1 = (f32[512]{0:T(512)S(1)}, f32[512]{0:T(512)}, u32[]{:S(2)}) copy-start(f32[512]{0:T(512)} %param.8) | copy-start | bytes 6148
  112.6 0.7 copy-start.2
Sparse Core Ops, SparseCore 0:
  8.9 94.0 all-gather.1
  112.8 171.9 all-reduce.2
